TPU v7x, 32 devices: a whole 2x2x4 slice. The times are simulated.
32 devices in a mesh: rep: 16 (over z, x, core), slab: 2 (over y).
Axes of the slice: x: 2, y: 2, z: 4, core: 2. Of those that a mesh axis runs over, the one named last changes fastest.
Arguments:
- weights: bfloat16 [16, 256, 3072], P('rep', 'slab'), may hold values from -6 to 6
- perms: int32 [16, 8, 256], P('rep'), may hold values from 0 to 255, each once within a row
Outputs:
- merged: bfloat16 [16, 256, 3072], P('rep', 'slab')
Inputs may be any that keep to these rules, and one draw needn't show every extreme that they name: `perms`: each row of 256 entries names every neuron of the window once.
All inputs are finite; a program needn't handle non-finite values.
Results may differ from a plain program's by a relative error of at most 0.012.
Values may be sent and summed in bfloat16 or wider, within the bound.
A program may use at most 64 MiB of HBM per device.

v0:
```python
import math
import jax
import jax.numpy as jnp
from jax import lax
from jax.sharding import PartitionSpec as P

D = 3072
ROUNDS = 8


def from_partner(x, axis, stride):
    return lax.ppermute(x, axis, [(i, i ^ 1 << stride) for i in range(lax.axis_size(axis))])


def finish_round(own, partner, perm_rows, cost):
    squared = cost * cost
    fourth = squared * squared
    soft_plan = fourth / (1.0 + jnp.sum(fourth, axis=1, keepdims=True))
    columns = jnp.arange(partner.shape[0], dtype=jnp.int32)
    onehot = (perm_rows[:, None] == columns[None, :]).astype(jnp.float32)
    mixing = (onehot + soft_plan).astype(jnp.bfloat16)
    aligned = 0.5 * jnp.dot(mixing, partner, preferred_element_type=jnp.float32)
    return ((own.astype(jnp.float32) + aligned) * (1.0 / math.sqrt(2.0))).astype(jnp.bfloat16)


def local(weights, perms):
    bit_count = lax.axis_size("rep").bit_length() - 1
    current = weights[0]
    perm_plan = perms[0]
    feature_part = lax.all_to_all(current, "slab", split_axis=1, concat_axis=0, tiled=True)
    for round_idx in range(ROUNDS):
        partner = from_partner(feature_part, "rep", round_idx % bit_count)
        partial_value = jnp.dot(feature_part, partner.T, preferred_element_type=jnp.float32)
        cost = lax.psum(partial_value, "slab") * (1.0 / math.sqrt(D))
        feature_part = finish_round(feature_part, partner, perm_plan[round_idx], cost)
    result = lax.all_to_all(feature_part, "slab", split_axis=0, concat_axis=1, tiled=True)
    return result[None]


def solution(mesh):
    placed = (P("rep", "slab", None), P("rep", None, None))
    return jax.shard_map(
        local, mesh=mesh, in_specs=placed, out_specs=P("rep", "slab", None), check_vma=False
    )
```

profile of v0, /device:TPU:0, one launch (start us, length us, event | category | flops | bytes accessed | tf_op | source)
XLA Modules:
  0.0 416.3 jit_solution(1840238187815374392)
XLA Ops:
  6.5 2.6 all_to_all.26
  9.2 14.8 %all_to_all.35 = bf16[128,2,1536]{2,0,1:T(8,128)(2,1)S(1)} all-to-all(bf16[128,2,1536]{2,0,1:T(8,128)(2,1)S(1)} %copy.3), channel_id=1, replica_groups=mesh['rep'=16,'slab'=2] {'slab'}, dimensions={1} | all-to-all | bytes 1572864 | tf_op jit(solution)/shard_map/all_to_all | solution.py:30
  24.0 2.3 collective-permute-done
  27.5 23.8 %all-reduce.9.cloned.1.call-done = f32[256,256]{1,0:T(8,128)} async-done(((f32[256,256]{1,0:T(8,128)}), f32[256,256]{1,0:T(8,128)}) %all-reduce.9.cloned.1.call-update) | async-done | bytes 262160 | tf_op jit(solution)/shard_map/psum | solution.py:34
  55.4 17.3 %collective-permute-done.1 = bf16[256,1536]{1,0:T(8,128)(2,1)S(1)} collective-permute-done((bf16[256,1536]{1,0:T(8,128)(2,1)S(1)}, bf16[256,1536]{1,0:T(8,128)(2,1)S(1)}, u32[]{:S(2)}, u32[]{:S(2)}) %collective-permute-start.1) | collective-permute-done | bytes 786464 | tf_op jit(solution)/shard_map/ppermute | solution.py:12
  73.8 23.4 %all-reduce.11.cloned.1.call-done = f32[256,256]{1,0:T(8,128)} async-done(((f32[256,256]{1,0:T(8,128)}), f32[256,256]{1,0:T(8,128)}) %all-reduce.11.cloned.1.call-update) | async-done | bytes 262160 | tf_op jit(solution)/shard_map/psum | solution.py:34
  99.7 1.6 collective-permute-start.2
  101.3 17.3 %collective-permute-done.2 = bf16[256,1536]{1,0:T(8,128)(2,1)S(1)} collective-permute-done((bf16[256,1536]{1,0:T(8,128)(2,1)S(1)}, bf16[256,1536]{1,0:T(8,128)(2,1)S(1)}, u32[]{:S(2)}, u32[]{:S(2)}) %collective-permute-start.2) | collective-permute-done | bytes 786464 | tf_op jit(solution)/shard_map/ppermute | solution.py:12
  119.8 23.4 %all-reduce.13.cloned.1.call-done = f32[256,256]{1,0:T(8,128)} async-done(((f32[256,256]{1,0:T(8,128)}), f32[256,256]{1,0:T(8,128)}) %all-reduce.13.cloned.1.call-update) | async-done | bytes 262160 | tf_op jit(solution)/shard_map/psum | solution.py:34
  145.7 2.5 collective-permute-start.3
  148.1 34.1 %collective-permute-done.3 = bf16[256,1536]{1,0:T(8,128)(2,1)S(1)} collective-permute-done((bf16[256,1536]{1,0:T(8,128)(2,1)S(1)}, bf16[256,1536]{1,0:T(8,128)(2,1)S(1)}, u32[]{:S(2)}, u32[]{:S(2)}) %collective-permute-start.3) | collective-permute-done | bytes 786464 | tf_op jit(solution)/shard_map/ppermute | solution.py:12
  183.4 23.4 %all-reduce.15.cloned.1.call-done = f32[256,256]{1,0:T(8,128)} async-done(((f32[256,256]{1,0:T(8,128)}), f32[256,256]{1,0:T(8,128)}) %all-reduce.15.cloned.1.call-update) | async-done | bytes 262160 | tf_op jit(solution)/shard_map/psum | solution.py:34
  209.4 2.3 collective-permute-done.4
  212.8 23.4 %all-reduce.17.cloned.1.call-done = f32[256,256]{1,0:T(8,128)} async-done(((f32[256,256]{1,0:T(8,128)}), f32[256,256]{1,0:T(8,128)}) %all-reduce.17.cloned.1.call-update) | async-done | bytes 262160 | tf_op jit(solution)/shard_map/psum | solution.py:34
  238.7 1.5 collective-permute-start.5
  240.3 17.3 %collective-permute-done.5 = bf16[256,1536]{1,0:T(8,128)(2,1)S(1)} collective-permute-done((bf16[256,1536]{1,0:T(8,128)(2,1)S(1)}, bf16[256,1536]{1,0:T(8,128)(2,1)S(1)}, u32[]{:S(2)}, u32[]{:S(2)}) %collective-permute-start.5) | collective-permute-done | bytes 786464 | tf_op jit(solution)/shard_map/ppermute | solution.py:12
  258.8 23.4 %all-reduce.19.cloned.1.call-done = f32[256,256]{1,0:T(8,128)} async-done(((f32[256,256]{1,0:T(8,128)}), f32[256,256]{1,0:T(8,128)}) %all-reduce.19.cloned.1.call-update) | async-done | bytes 262160 | tf_op jit(solution)/shard_map/psum | solution.py:34
  284.7 1.6 collective-permute-start.6
  286.2 17.3 %collective-permute-done.6 = bf16[256,1536]{1,0:T(8,128)(2,1)S(1)} collective-permute-done((bf16[256,1536]{1,0:T(8,128)(2,1)S(1)}, bf16[256,1536]{1,0:T(8,128)(2,1)S(1)}, u32[]{:S(2)}, u32[]{:S(2)}) %collective-permute-start.6) | collective-permute-done | bytes 786464 | tf_op jit(solution)/shard_map/ppermute | solution.py:12
  304.7 23.4 %all-reduce.21.cloned.1.call-done = f32[256,256]{1,0:T(8,128)} async-done(((f32[256,256]{1,0:T(8,128)}), f32[256,256]{1,0:T(8,128)}) %all-reduce.21.cloned.1.call-update) | async-done | bytes 262160 | tf_op jit(solution)/shard_map/psum | solution.py:34
  330.6 2.5 collective-permute-start.7
  333.1 34.1 %collective-permute-done.7 = bf16[256,1536]{1,0:T(8,128)(2,1)S(1)} collective-permute-done((bf16[256,1536]{1,0:T(8,128)(2,1)S(1)}, bf16[256,1536]{1,0:T(8,128)(2,1)S(1)}, u32[]{:S(2)}, u32[]{:S(2)}) %collective-permute-start.7) | collective-permute-done | bytes 786464 | tf_op jit(solution)/shard_map/ppermute | solution.py:12
  368.3 23.4 %all-reduce.23.cloned.1.call-done = f32[256,256]{1,0:T(8,128)} async-done(((f32[256,256]{1,0:T(8,128)}), f32[256,256]{1,0:T(8,128)}) %all-reduce.23.cloned.1.call-update) | async-done | bytes 262160 | tf_op jit(solution)/shard_map/psum | solution.py:34
  394.2 13.0 %all_to_all.36 = bf16[2,128,1536]{2,1,0:T(8,128)(2,1)S(1)} all-to-all(bf16[2,128,1536]{2,1,0:T(8,128)(2,1)S(1)} %bitcast.41), channel_id=1, replica_groups=mesh['rep'=16,'slab'=2] {'slab'}, dimensions={0} | all-to-all | bytes 1572864 | tf_op jit(solution)/shard_map/all_to_all | solution.py:36
  (57 shorter events, 33.0 us)
Async XLA Ops:
  6.5 44.8 %all-reduce.9.cloned.1.call-start = ((), (), s32[]{:S(2)}) async-start(), calls=%async_computation.2 | async-start | bytes 524288 | tf_op jit(solution)/shard_map/psum | solution.py:34
  24.0 3.5 copy-start
  24.0 2.3 collective-permute-start
  27.5 69.8 %all-reduce.11.cloned.1.call-start = ((), (), s32[]{:S(2)}) async-start(), calls=%async_computation.3 | async-start | bytes 524288 | tf_op jit(solution)/shard_map/psum | solution.py:34
  53.8 18.8 %collective-permute-start.1 = (bf16[256,1536]{1,0:T(8,128)(2,1)S(1)}, bf16[256,1536]{1,0:T(8,128)(2,1)S(1)}, u32[]{:S(2)}, u32[]{:S(2)}) collective-permute-start(bf16[256,1536]{1,0:T(8,128)(2,1)S(1)} %fusion.16), channel_id=1, source_target_pairs={{0,4},{2,6},{4,0},{6,2},{8,12},{10,14},{12,8},{14,10},{16,20},{18,... | collective-permute-start | bytes 2359304 | tf_op jit(solution)/shard_map/ppermute | solution.py:12
  73.8 69.4 %all-reduce.13.cloned.1.call-start = ((), (), s32[]{:S(2)}) async-start(), calls=%async_computation.4 | async-start | bytes 524288 | tf_op jit(solution)/shard_map/psum | solution.py:34
  99.7 18.8 %collective-permute-start.2 = (bf16[256,1536]{1,0:T(8,128)(2,1)S(1)}, bf16[256,1536]{1,0:T(8,128)(2,1)S(1)}, u32[]{:S(2)}, u32[]{:S(2)}) collective-permute-start(bf16[256,1536]{1,0:T(8,128)(2,1)S(1)} %fusion.17), channel_id=1, source_target_pairs={{0,8},{2,10},{4,12},{6,14},{8,0},{10,2},{12,4},{14,6},{16,24},{18,... | collective-permute-start | bytes 2359304 | tf_op jit(solution)/shard_map/ppermute | solution.py:12
  119.7 87.1 %all-reduce.15.cloned.1.call-start = ((), (), s32[]{:S(2)}) async-start(), calls=%async_computation.5 | async-start | bytes 524288 | tf_op jit(solution)/shard_map/psum | solution.py:34
  145.7 36.6 %collective-permute-start.3 = (bf16[256,1536]{1,0:T(8,128)(2,1)S(1)}, bf16[256,1536]{1,0:T(8,128)(2,1)S(1)}, u32[]{:S(2)}, u32[]{:S(2)}) collective-permute-start(bf16[256,1536]{1,0:T(8,128)(2,1)S(1)} %fusion.18), channel_id=1, source_target_pairs={{0,16},{2,18},{4,20},{6,22},{8,24},{10,26},{12,28},{14,30},{16,0},... | collective-permute-start | bytes 2359304 | tf_op jit(solution)/shard_map/ppermute | solution.py:12
  183.4 52.9 %all-reduce.17.cloned.1.call-start = ((), (), s32[]{:S(2)}) async-start(), calls=%async_computation.6 | async-start | bytes 524288 | tf_op jit(solution)/shard_map/psum | solution.py:34
  209.3 2.4 collective-permute-start.4
  212.8 69.4 %all-reduce.19.cloned.1.call-start = ((), (), s32[]{:S(2)}) async-start(), calls=%async_computation.7 | async-start | bytes 524288 | tf_op jit(solution)/shard_map/psum | solution.py:34
  238.7 18.8 %collective-permute-start.5 = (bf16[256,1536]{1,0:T(8,128)(2,1)S(1)}, bf16[256,1536]{1,0:T(8,128)(2,1)S(1)}, u32[]{:S(2)}, u32[]{:S(2)}) collective-permute-start(bf16[256,1536]{1,0:T(8,128)(2,1)S(1)} %fusion.20), channel_id=1, source_target_pairs={{0,4},{2,6},{4,0},{6,2},{8,12},{10,14},{12,8},{14,10},{16,20},{18,... | collective-permute-start | bytes 2359304 | tf_op jit(solution)/shard_map/ppermute | solution.py:12
  258.7 69.4 %all-reduce.21.cloned.1.call-start = ((), (), s32[]{:S(2)}) async-start(), calls=%async_computation.8 | async-start | bytes 524288 | tf_op jit(solution)/shard_map/psum | solution.py:34
  284.7 18.8 %collective-permute-start.6 = (bf16[256,1536]{1,0:T(8,128)(2,1)S(1)}, bf16[256,1536]{1,0:T(8,128)(2,1)S(1)}, u32[]{:S(2)}, u32[]{:S(2)}) collective-permute-start(bf16[256,1536]{1,0:T(8,128)(2,1)S(1)} %fusion.21), channel_id=1, source_target_pairs={{0,8},{2,10},{4,12},{6,14},{8,0},{10,2},{12,4},{14,6},{16,24},{18,... | collective-permute-start | bytes 2359304 | tf_op jit(solution)/shard_map/ppermute | solution.py:12
  304.6 87.1 %all-reduce.23.cloned.1.call-start = ((), (), s32[]{:S(2)}) async-start(), calls=%async_computation.9 | async-start | bytes 524288 | tf_op jit(solution)/shard_map/psum | solution.py:34
  330.6 36.6 %collective-permute-start.7 = (bf16[256,1536]{1,0:T(8,128)(2,1)S(1)}, bf16[256,1536]{1,0:T(8,128)(2,1)S(1)}, u32[]{:S(2)}, u32[]{:S(2)}) collective-permute-start(bf16[256,1536]{1,0:T(8,128)(2,1)S(1)} %fusion.22), channel_id=1, source_target_pairs={{0,16},{2,18},{4,20},{6,22},{8,24},{10,26},{12,28},{14,30},{16,0},... | collective-permute-start | bytes 2359304 | tf_op jit(solution)/shard_map/ppermute | solution.py:12
Sparse Core Ops, SparseCore 0:
  27.6 23.7 all-reduce.8
  73.9 23.2 all-reduce.10
  119.8 23.2 all-reduce.12
  183.5 23.2 all-reduce.14
  212.9 23.2 all-reduce.16
  258.8 23.2 all-reduce.18
  304.7 23.2 all-reduce.20
  368.4 23.2 all-reduce.22
where the time goes:
time: 417 us; the launch traced here: 416 us
  waiting for transfers between devices  330 us (79%)
  blocking collectives  27.8 us (7%)
  matrix products  20.1 us (5%)
  between operations  13.7 us (3%)
  starting transfers between devices  11.5 us (3%)
  other arithmetic  8.54 us (2%)
  local copies, waits for them, and re-layouts  4.93 us (1%)
    psum x8, waiting for transfers between devices, local(): cost = lax.psum(partial_value, 'slab') * (1.0 / math.sqrt(D))  188 us
    ppermute x8, waiting for transfers between devices, from_partner(): lax.ppermute(x, axis, [(i, i ^ 1 << stride) for i in range(lax.axis_size(...  142 us
    all_to_all x1, blocking collectives, local(): lax.all_to_all(current, 'slab', split_axis=1, concat_axis=0, tiled=True)  14.8 us
    all_to_all x1, blocking collectives, local(): lax.all_to_all(feature_part, 'slab', split_axis=0, concat_axis=1, tiled=T...  13 us
    dot_general x8, matrix products, finish_round(): aligned = 0.5 * jnp.dot(mixing, partner, preferred_element_type=jnp.float32)  11.2 us
    ppermute x8, starting transfers between devices, from_partner(): lax.ppermute(x, axis, [(i, i ^ 1 << stride) for i in range(lax.axis_size(...  11.2 us
    dot_general x8, matrix products, local(): jnp.dot(feature_part, partner.T, preferred_element_type=jnp.float32)  8.84 us
    reduce_sum x8, other arithmetic, finish_round(): soft_plan = fourth / (1.0 + jnp.sum(fourth, axis=1, keepdims=True))  8.51 us
  transfers between devices with their start and end apart: 16, of which 16 were waited for; matrix products, arithmetic and copies ran while one was open for 0% of the time, Pallas kernels for 0%

commit v1 on v0

--- a/solution.py
+++ b/solution.py
@@ -31,7 +31,7 @@
     for round_idx in range(ROUNDS):
         partner = from_partner(feature_part, "rep", round_idx % bit_count)
         partial_value = jnp.dot(feature_part, partner.T, preferred_element_type=jnp.float32)
-        cost = lax.psum(partial_value, "slab") * (1.0 / math.sqrt(D))
+        cost = jnp.sum(lax.all_gather(partial_value, "slab"), axis=0) * (1.0 / math.sqrt(D))
         feature_part = finish_round(feature_part, partner, perm_plan[round_idx], cost)
     result = lax.all_to_all(feature_part, "slab", split_axis=0, concat_axis=1, tiled=True)
     return result[None]

time: 417 us -> 246 us (0.59)
  waiting for transfers between devices: 330 us -> 130 us
  blocking collectives: 27.8 us -> 89.3 us
  between operations: 13.7 us -> 0.29 us
  matrix products: 20.1 us -> 6.83 us
  other arithmetic: 8.54 us -> 1.22 us
    psum x8 -> x0, waiting for transfers between devices: 188 us -> none  [local(): cost = lax.psum(partial_value, 'slab') * (1.0 / math.sqrt(D))]
    all_gather x0 -> x8, blocking collectives: none -> 62.6 us  [local(): lax.all_gather(partial_value, 'slab')]
    ppermute x8, waiting for transfers between devices: 142 us -> 130 us  [from_partner(): lax.ppermute(x, axis, [(i, i ^ 1 << stride) for i in range(lax.axis_size(...]
    reduce_sum x8, other arithmetic: 8.51 us -> 0.92 us  [finish_round(): soft_plan = fourth / (1.0 + jnp.sum(fourth, axis=1, keepdims=True))]
    dot_general x8, matrix products: 11.2 us -> 3.66 us  [finish_round(): aligned = 0.5 * jnp.dot(mixing, partner, preferred_element_type=jnp.float32)]
    dot_general x8, matrix products: 8.84 us -> 3.17 us  [local(): jnp.dot(feature_part, partner.T, preferred_element_type=jnp.float32)]
  transfers between devices with their start and end apart: 16 -> 8, of which waited for: 16 -> 8; matrix products, arithmetic and copies ran while one was open for 0% -> 0% of each run, Pallas kernels for 0% -> 0%
where the time goes in v1:
time: 246 us
  waiting for transfers between devices  130 us (53%)
  blocking collectives  89.3 us (36%)
  starting transfers between devices  13.2 us (5%)
  matrix products  6.83 us (3%)
  local copies, waits for them, and re-layouts  4.93 us (2%)
    ppermute x8, waiting for transfers between devices, from_partner(): lax.ppermute(x, axis, [(i, i ^ 1 << stride) for i in range(lax.axis_size(...  130 us
    all_gather x8, blocking collectives, local(): lax.all_gather(partial_value, 'slab')  62.6 us
    all_to_all x1, blocking collectives, local(): lax.all_to_all(current, 'slab', split_axis=1, concat_axis=0, tiled=True)  14.8 us
    ppermute x8, starting transfers between devices, from_partner(): lax.ppermute(x, axis, [(i, i ^ 1 << stride) for i in range(lax.axis_size(...  13.2 us
    all_to_all x1, blocking collectives, local(): lax.all_to_all(feature_part, 'slab', split_axis=0, concat_axis=1, tiled=T...  11.9 us
  transfers between devices with their start and end apart: 8, of which 8 were waited for; matrix products, arithmetic and copies ran while one was open for 0% of the time, Pallas kernels for 0%

profile of v1, /device:TPU:0, one launch (start us, length us, event | category | flops | bytes accessed | tf_op | source)
XLA Modules:
  0.0 245.7 jit_solution(9858181487348465004)
XLA Ops:
  0.0 2.6 %all_to_all.26 = bf16[128,2,1536]{2,1,0:T(2,128)(2,1)S(1)} reshape(bf16[1,128,3072]{2,1,0:T(8,128)(2,1)} %param.2) | data formatting | bytes 1572864 | tf_op jit(solution)/shard_map/all_to_all | solution.py:30
  2.7 14.8 %all_to_all.35 = bf16[128,2,1536]{2,0,1:T(8,128)(2,1)S(1)} all-to-all(bf16[128,2,1536]{2,0,1:T(8,128)(2,1)S(1)} %copy.5), channel_id=1, replica_groups=mesh['rep'=16,'slab'=2] {'slab'}, dimensions={1} | all-to-all | bytes 1572864 | tf_op jit(solution)/shard_map/all_to_all | solution.py:30
  17.5 2.3 collective-permute-done
  20.2 9.0 %all-gather = f32[512,256]{1,0:T(8,128)S(1)} all-gather(f32[256,256]{1,0:T(8,128)S(1)} %fusion.65), channel_id=2, replica_groups=mesh['rep'=16,'slab'=2] {'slab'}, dimensions={0}, use_global_device_ids=true | all-gather | bytes 786432 | tf_op jit(solution)/shard_map/all_gather | solution.py:34
  29.9 1.7 collective-permute-start.1
  31.5 17.1 %collective-permute-done.1 = bf16[256,1536]{1,0:T(8,128)(2,1)S(1)} collective-permute-done((bf16[256,1536]{1,0:T(8,128)(2,1)S(1)}, bf16[256,1536]{1,0:T(8,128)(2,1)S(1)}, u32[]{:S(2)}, u32[]{:S(2)}) %collective-permute-start.1) | collective-permute-done | bytes 786464 | tf_op jit(solution)/shard_map/ppermute | solution.py:12
  49.0 7.3 %all-gather.1 = f32[512,256]{1,0:T(8,128)S(1)} all-gather(f32[256,256]{1,0:T(8,128)S(1)} %fusion.66), channel_id=3, replica_groups=mesh['rep'=16,'slab'=2] {'slab'}, dimensions={0}, use_global_device_ids=true | all-gather | bytes 786432 | tf_op jit(solution)/shard_map/all_gather | solution.py:34
  57.0 1.8 collective-permute-start.2
  58.7 15.3 %collective-permute-done.2 = bf16[256,1536]{1,0:T(8,128)(2,1)S(1)} collective-permute-done((bf16[256,1536]{1,0:T(8,128)(2,1)S(1)}, bf16[256,1536]{1,0:T(8,128)(2,1)S(1)}, u32[]{:S(2)}, u32[]{:S(2)}) %collective-permute-start.2) | collective-permute-done | bytes 786464 | tf_op jit(solution)/shard_map/ppermute | solution.py:12
  74.5 7.0 %all-gather.2 = f32[512,256]{1,0:T(8,128)S(1)} all-gather(f32[256,256]{1,0:T(8,128)S(1)} %fusion.67), channel_id=4, replica_groups=mesh['rep'=16,'slab'=2] {'slab'}, dimensions={0}, use_global_device_ids=true | all-gather | bytes 786432 | tf_op jit(solution)/shard_map/all_gather | solution.py:34
  82.1 2.8 %collective-permute-start.3 = (bf16[256,1536]{1,0:T(8,128)(2,1)S(1)}, bf16[256,1536]{1,0:T(8,128)(2,1)S(1)}, u32[]{:S(2)}, u32[]{:S(2)}) collective-permute-start(bf16[256,1536]{1,0:T(8,128)(2,1)S(1)} %fusion.18), channel_id=1, source_target_pairs={{0,16},{2,18},{4,20},{6,22},{8,24},{10,26},{12,28},{14,30},{16,0},... | collective-permute-start | bytes 2359304 | tf_op jit(solution)/shard_map/ppermute | solution.py:12
  84.9 30.1 %collective-permute-done.3 = bf16[256,1536]{1,0:T(8,128)(2,1)S(1)} collective-permute-done((bf16[256,1536]{1,0:T(8,128)(2,1)S(1)}, bf16[256,1536]{1,0:T(8,128)(2,1)S(1)}, u32[]{:S(2)}, u32[]{:S(2)}) %collective-permute-start.3) | collective-permute-done | bytes 786464 | tf_op jit(solution)/shard_map/ppermute | solution.py:12
  115.4 7.9 %all-gather.3 = f32[512,256]{1,0:T(8,128)S(1)} all-gather(f32[256,256]{1,0:T(8,128)S(1)} %fusion.68), channel_id=5, replica_groups=mesh['rep'=16,'slab'=2] {'slab'}, dimensions={0}, use_global_device_ids=true | all-gather | bytes 786432 | tf_op jit(solution)/shard_map/all_gather | solution.py:34
  124.0 2.3 collective-permute-done.4
  126.7 9.0 %all-gather.4 = f32[512,256]{1,0:T(8,128)S(1)} all-gather(f32[256,256]{1,0:T(8,128)S(1)} %fusion.69), channel_id=6, replica_groups=mesh['rep'=16,'slab'=2] {'slab'}, dimensions={0}, use_global_device_ids=true | all-gather | bytes 786432 | tf_op jit(solution)/shard_map/all_gather | solution.py:34
  137.9 17.2 %collective-permute-done.5 = bf16[256,1536]{1,0:T(8,128)(2,1)S(1)} collective-permute-done((bf16[256,1536]{1,0:T(8,128)(2,1)S(1)}, bf16[256,1536]{1,0:T(8,128)(2,1)S(1)}, u32[]{:S(2)}, u32[]{:S(2)}) %collective-permute-start.5) | collective-permute-done | bytes 786464 | tf_op jit(solution)/shard_map/ppermute | solution.py:12
  155.5 7.3 %all-gather.5 = f32[512,256]{1,0:T(8,128)S(1)} all-gather(f32[256,256]{1,0:T(8,128)S(1)} %fusion.70), channel_id=7, replica_groups=mesh['rep'=16,'slab'=2] {'slab'}, dimensions={0}, use_global_device_ids=true | all-gather | bytes 786432 | tf_op jit(solution)/shard_map/all_gather | solution.py:34
  163.5 1.8 collective-permute-start.6
  165.3 15.3 %collective-permute-done.6 = bf16[256,1536]{1,0:T(8,128)(2,1)S(1)} collective-permute-done((bf16[256,1536]{1,0:T(8,128)(2,1)S(1)}, bf16[256,1536]{1,0:T(8,128)(2,1)S(1)}, u32[]{:S(2)}, u32[]{:S(2)}) %collective-permute-start.6) | collective-permute-done | bytes 786464 | tf_op jit(solution)/shard_map/ppermute | solution.py:12
  181.0 7.0 %all-gather.6 = f32[512,256]{1,0:T(8,128)S(1)} all-gather(f32[256,256]{1,0:T(8,128)S(1)} %fusion.71), channel_id=8, replica_groups=mesh['rep'=16,'slab'=2] {'slab'}, dimensions={0}, use_global_device_ids=true | all-gather | bytes 786432 | tf_op jit(solution)/shard_map/all_gather | solution.py:34
  188.6 3.4 %collective-permute-start.7 = (bf16[256,1536]{1,0:T(8,128)(2,1)S(1)}, bf16[256,1536]{1,0:T(8,128)(2,1)S(1)}, u32[]{:S(2)}, u32[]{:S(2)}) collective-permute-start(bf16[256,1536]{1,0:T(8,128)(2,1)S(1)} %fusion.22), channel_id=1, source_target_pairs={{0,16},{2,18},{4,20},{6,22},{8,24},{10,26},{12,28},{14,30},{16,0},... | collective-permute-start | bytes 2359304 | tf_op jit(solution)/shard_map/ppermute | solution.py:12
  192.1 30.4 %collective-permute-done.7 = bf16[256,1536]{1,0:T(8,128)(2,1)S(1)} collective-permute-done((bf16[256,1536]{1,0:T(8,128)(2,1)S(1)}, bf16[256,1536]{1,0:T(8,128)(2,1)S(1)}, u32[]{:S(2)}, u32[]{:S(2)}) %collective-permute-start.7) | collective-permute-done | bytes 786464 | tf_op jit(solution)/shard_map/ppermute | solution.py:12
  222.8 8.0 %all-gather.7 = f32[512,256]{1,0:T(8,128)S(1)} all-gather(f32[256,256]{1,0:T(8,128)S(1)} %fusion.72), channel_id=9, replica_groups=mesh['rep'=16,'slab'=2] {'slab'}, dimensions={0}, use_global_device_ids=true | all-gather | bytes 786432 | tf_op jit(solution)/shard_map/all_gather | solution.py:34
  231.5 11.9 %all_to_all.36 = bf16[2,128,1536]{2,1,0:T(8,128)(2,1)S(1)} all-to-all(bf16[2,128,1536]{2,1,0:T(8,128)(2,1)S(1)} %bitcast.57), channel_id=1, replica_groups=mesh['rep'=16,'slab'=2] {'slab'}, dimensions={0} | all-to-all | bytes 1572864 | tf_op jit(solution)/shard_map/all_to_all | solution.py:36
  (49 shorter events, 12.1 us)
Async XLA Ops:
  2.7 14.9 %copy-start = (s32[1,8,256]{2,1,0:T(8,128)S(1)}, s32[1,8,256]{2,1,0:T(8,128)}, u32[]{:S(2)}) copy-start(s32[1,8,256]{2,1,0:T(8,128)} %param.3) | copy-start | bytes 24580
  17.5 2.3 collective-permute-start
  29.9 18.8 %collective-permute-start.1 = (bf16[256,1536]{1,0:T(8,128)(2,1)S(1)}, bf16[256,1536]{1,0:T(8,128)(2,1)S(1)}, u32[]{:S(2)}, u32[]{:S(2)}) collective-permute-start(bf16[256,1536]{1,0:T(8,128)(2,1)S(1)} %fusion.16), channel_id=1, source_target_pairs={{0,4},{2,6},{4,0},{6,2},{8,12},{10,14},{12,8},{14,10},{16,20},{18,... | collective-permute-start | bytes 2359304 | tf_op jit(solution)/shard_map/ppermute | solution.py:12
  57.0 17.1 %collective-permute-start.2 = (bf16[256,1536]{1,0:T(8,128)(2,1)S(1)}, bf16[256,1536]{1,0:T(8,128)(2,1)S(1)}, u32[]{:S(2)}, u32[]{:S(2)}) collective-permute-start(bf16[256,1536]{1,0:T(8,128)(2,1)S(1)} %fusion.17), channel_id=1, source_target_pairs={{0,8},{2,10},{4,12},{6,14},{8,0},{10,2},{12,4},{14,6},{16,24},{18,... | collective-permute-start | bytes 2359304 | tf_op jit(solution)/shard_map/ppermute | solution.py:12
  82.1 32.9 %collective-permute-start.3 = (bf16[256,1536]{1,0:T(8,128)(2,1)S(1)}, bf16[256,1536]{1,0:T(8,128)(2,1)S(1)}, u32[]{:S(2)}, u32[]{:S(2)}) collective-permute-start(bf16[256,1536]{1,0:T(8,128)(2,1)S(1)} %fusion.18), channel_id=1, source_target_pairs={{0,16},{2,18},{4,20},{6,22},{8,24},{10,26},{12,28},{14,30},{16,0},... | collective-permute-start | bytes 2359304 | tf_op jit(solution)/shard_map/ppermute | solution.py:12
  123.9 2.4 collective-permute-start.4
  136.3 18.8 %collective-permute-start.5 = (bf16[256,1536]{1,0:T(8,128)(2,1)S(1)}, bf16[256,1536]{1,0:T(8,128)(2,1)S(1)}, u32[]{:S(2)}, u32[]{:S(2)}) collective-permute-start(bf16[256,1536]{1,0:T(8,128)(2,1)S(1)} %fusion.20), channel_id=1, source_target_pairs={{0,4},{2,6},{4,0},{6,2},{8,12},{10,14},{12,8},{14,10},{16,20},{18,... | collective-permute-start | bytes 2359304 | tf_op jit(solution)/shard_map/ppermute | solution.py:12
  163.5 17.1 %collective-permute-start.6 = (bf16[256,1536]{1,0:T(8,128)(2,1)S(1)}, bf16[256,1536]{1,0:T(8,128)(2,1)S(1)}, u32[]{:S(2)}, u32[]{:S(2)}) collective-permute-start(bf16[256,1536]{1,0:T(8,128)(2,1)S(1)} %fusion.21), channel_id=1, source_target_pairs={{0,8},{2,10},{4,12},{6,14},{8,0},{10,2},{12,4},{14,6},{16,24},{18,... | collective-permute-start | bytes 2359304 | tf_op jit(solution)/shard_map/ppermute | solution.py:12
  188.6 33.8 %collective-permute-start.7 = (bf16[256,1536]{1,0:T(8,128)(2,1)S(1)}, bf16[256,1536]{1,0:T(8,128)(2,1)S(1)}, u32[]{:S(2)}, u32[]{:S(2)}) collective-permute-start(bf16[256,1536]{1,0:T(8,128)(2,1)S(1)} %fusion.22), channel_id=1, source_target_pairs={{0,16},{2,18},{4,20},{6,22},{8,24},{10,26},{12,28},{14,30},{16,0},... | collective-permute-start | bytes 2359304 | tf_op jit(solution)/shard_map/ppermute | solution.py:12
